TPU v7x, 32 devices: a whole 2x2x4 slice. The times are simulated.
32 devices in a mesh: elem: 8 (over z, y), chan: 4 (over x, core).
Axes of the slice: x: 2, y: 2, z: 4, core: 2. Of those that a mesh axis runs over, the one named last changes fastest.
Arguments:
- voltages: bfloat16 [2, 1024, 19584], P(None, ('elem', 'chan')), may hold values from -6 to 6
- delays: int32 [1024], P(('elem', 'chan')), may hold values from 0 to 127
- prototype: bfloat16 [16, 1024], replicated, may hold values from -1.5 to 1.5
- subband_map: int32 [16], replicated, may hold values from 0 to 1023, as said below
- beam_weights: bfloat16 [512, 2, 16, 1024], P('elem', None, 'chan'), may hold values from -0.25 to 0.25
Outputs:
- element_power: bfloat16 [1024, 1024], P(('elem', 'chan'))
- beam_voltages: float32 [2, 64, 512], P(None, 'chan', 'elem')
Inputs may be any that keep to these rules, and one draw needn't show every extreme that they name: `subband_map`: distinct channel numbers.
All inputs are finite; a program needn't handle non-finite values.
Results may differ from a plain program's by a relative error of at most 0.007.
Values may be sent and summed in bfloat16 or wider, within the bound.
A program may use at most 128 MiB of HBM per device.

v0:
```python
import math
import jax
import jax.numpy as jnp
from jax import lax
from jax.sharding import PartitionSpec as P

FRAMES = 4
SUB_C = 4


def filtered(voltages, delays, prototype):
    tap_count, chan_count = prototype.shape
    blocks = FRAMES + tap_count - 1
    window_len = blocks * chan_count

    def window(samples, offset):
        return lax.dynamic_slice_in_dim(samples, offset, window_len, 0)

    segments = jax.vmap(jax.vmap(window, in_axes=(0, 0)), in_axes=(0, None))(voltages, delays)
    segments = segments.reshape(voltages.shape[0], voltages.shape[1], blocks, chan_count)
    coeffs = prototype.astype(jnp.float32)
    running = jnp.zeros((voltages.shape[0], voltages.shape[1], FRAMES, chan_count), jnp.float32)
    for tap_index in range(tap_count):
        running = running + coeffs[tap_index] * segments[
            :, :, tap_index : tap_index + FRAMES, :
        ].astype(jnp.float32)
    return running.astype(jnp.bfloat16)


def spectra(filtered_wave):
    part_count, elem_count, frame_count, chan_count = filtered_wave.shape
    counter = jnp.arange(chan_count, dtype=jnp.int32)
    residue = counter[:, None] * counter[None, :] % chan_count
    radians = residue.astype(jnp.float32) * (2.0 * math.pi / chan_count)
    factor = 1.0 / math.sqrt(chan_count)
    basis = jnp.concatenate([jnp.cos(radians) * factor, jnp.sin(radians) * factor], axis=1)
    basis_high = basis.astype(jnp.bfloat16)
    basis_low = (basis - basis_high.astype(jnp.float32)).astype(jnp.bfloat16)
    flattened = filtered_wave.reshape(part_count * elem_count * frame_count, chan_count)
    product = jnp.dot(flattened, basis_high, preferred_element_type=jnp.float32)
    product = product + jnp.dot(flattened, basis_low, preferred_element_type=jnp.float32)
    product = product.reshape(part_count, elem_count, frame_count, 2, chan_count)
    spec_real = product[0, :, :, 0] + product[1, :, :, 1]
    spec_imag = product[1, :, :, 0] - product[0, :, :, 1]
    return (spec_real, spec_imag)


def beam_terms(spectra_part, weight_part):
    weight_real = weight_part[:, 0]
    weight_imag = weight_part[:, 1]

    def contract(spectral, weighting):
        return jnp.einsum("sfe,bse->sfb", spectral, weighting, preferred_element_type=jnp.float32)

    out_real = contract(spectra_part[0], weight_real) - contract(spectra_part[1], weight_imag)
    out_imag = contract(spectra_part[1], weight_real) + contract(spectra_part[0], weight_imag)
    return jnp.stack([out_real, out_imag])


def on_device(voltages, delays, prototype, subband_map, beam_weights):
    filtered_wave = filtered(voltages, delays, prototype)
    spec_real, spec_imag = spectra(filtered_wave)
    element_power = jnp.mean(spec_real * spec_real + spec_imag * spec_imag, axis=1).astype(
        jnp.bfloat16
    )
    picked = jnp.stack([spec_real[:, :, subband_map], spec_imag[:, :, subband_map]]).astype(
        jnp.bfloat16
    )
    picked = jnp.transpose(picked, (0, 3, 2, 1))
    turned = lax.all_to_all(picked, "chan", split_axis=1, concat_axis=3, tiled=True)
    local_beams = beam_weights.shape[0]
    summed = beam_terms(lax.all_gather(turned, "elem", axis=3, tiled=True), beam_weights)
    beam_voltages = summed.reshape(2, SUB_C * FRAMES, local_beams)
    return (element_power, beam_voltages)


def solution(mesh):
    return jax.shard_map(
        on_device,
        mesh=mesh,
        in_specs=(
            P(None, ("elem", "chan"), None),
            P(("elem", "chan")),
            P(),
            P(),
            P("elem", None, "chan", None),
        ),
        out_specs=(P(("elem", "chan"), None), P(None, "chan", "elem")),
        check_vma=False,
    )
```

profile of v0, /device:TPU:0, one launch (start us, length us, event | category | flops | bytes accessed | tf_op | source)
XLA Modules:
  0.0 187.4 jit_solution(4113093099833259249)
XLA Ops:
  0.7 17.8 %sine_multiply_fusion = (f32[1024,1024]{1,0:T(8,128)}, f32[1024,1024]{1,0:T(8,128)}) fusion(), kind=kLoop, calls=%fused_computation.14 | loop fusion | flops 16777216 | bytes 8388608 | tf_op jit(solution)/shard_map/mul | solution.py:36
  18.5 1.9 %copy.22 = bf16[2,32,19584]{2,0,1:T(2,128)(2,1)S(1)} copy(bf16[2,32,19584]{2,1,0:T(8,128)(2,1)S(1)} %copy-done.2) | data formatting | bytes 5013504
  20.5 85.7 %while.1 = (s32[]{:T(128)}, bf16[2,32,19584]{2,0,1:T(2,128)(2,1)S(1)}, s32[32,2]{0,1:T(2,128)S(1)}, bf16[32,2,19456]{2,1,0:T(2,128)(2,1)}, s32[]{:T(128)}) while((s32[]{:T(128)}, bf16[2,32,19584]{2,0,1:T(2,128)(2,1)S(1)}, s32[32,2]{0,1:T(2,128)S(1)}, bf16[32,2,19456]{2,1,0:T(2,128)(2,1)}, s32[]{:T(128)}) %tuple.49), condition=%wide.while_cond, body=%wide.while_body.sunk | while | flops 2 | bytes 157281 | solution.py:17
  21.2 2.1 %bitcast_dynamic-update-slice_fusion.2 = bf16[32,2,19456]{2,1,0:T(2,128)(2,1)} fusion(bf16[32,2,19456]{2,1,0:T(2,128)(2,1)} %get-tuple-element.97, s32[]{:T(128)} %get-tuple-element.94, bf16[2,32,19584]{2,0,1:T(2,128)(2,1)S(1)} %get-tuple-element.100, s32[]{:T(128)} %bitcast.72, s32[]{:T(128)} %bitcast.73), kind=kLoop, calls=%fused_computation.2.clone.1 | loop fusion | bytes 157184 | tf_op jit(solution)/shard_map/vmap(vmap())/gather
  23.8 2.1 %bitcast_dynamic-update-slice_fusion.2 = bf16[32,2,19456]{2,1,0:T(2,128)(2,1)} fusion(bf16[32,2,19456]{2,1,0:T(2,128)(2,1)} %get-tuple-element.97, s32[]{:T(128)} %get-tuple-element.94, bf16[2,32,19584]{2,0,1:T(2,128)(2,1)S(1)} %get-tuple-element.100, s32[]{:T(128)} %bitcast.72, s32[]{:T(128)} %bitcast.73), kind=kLoop, calls=%fused_computation.2.clone.1 | loop fusion | bytes 157184 | tf_op jit(solution)/shard_map/vmap(vmap())/gather
  26.5 2.1 %bitcast_dynamic-update-slice_fusion.2 = bf16[32,2,19456]{2,1,0:T(2,128)(2,1)} fusion(bf16[32,2,19456]{2,1,0:T(2,128)(2,1)} %get-tuple-element.97, s32[]{:T(128)} %get-tuple-element.94, bf16[2,32,19584]{2,0,1:T(2,128)(2,1)S(1)} %get-tuple-element.100, s32[]{:T(128)} %bitcast.72, s32[]{:T(128)} %bitcast.73), kind=kLoop, calls=%fused_computation.2.clone.1 | loop fusion | bytes 157184 | tf_op jit(solution)/shard_map/vmap(vmap())/gather
  29.2 2.1 %bitcast_dynamic-update-slice_fusion.2 = bf16[32,2,19456]{2,1,0:T(2,128)(2,1)} fusion(bf16[32,2,19456]{2,1,0:T(2,128)(2,1)} %get-tuple-element.97, s32[]{:T(128)} %get-tuple-element.94, bf16[2,32,19584]{2,0,1:T(2,128)(2,1)S(1)} %get-tuple-element.100, s32[]{:T(128)} %bitcast.72, s32[]{:T(128)} %bitcast.73), kind=kLoop, calls=%fused_computation.2.clone.1 | loop fusion | bytes 157184 | tf_op jit(solution)/shard_map/vmap(vmap())/gather
  31.9 2.1 %bitcast_dynamic-update-slice_fusion.2 = bf16[32,2,19456]{2,1,0:T(2,128)(2,1)} fusion(bf16[32,2,19456]{2,1,0:T(2,128)(2,1)} %get-tuple-element.97, s32[]{:T(128)} %get-tuple-element.94, bf16[2,32,19584]{2,0,1:T(2,128)(2,1)S(1)} %get-tuple-element.100, s32[]{:T(128)} %bitcast.72, s32[]{:T(128)} %bitcast.73), kind=kLoop, calls=%fused_computation.2.clone.1 | loop fusion | bytes 157184 | tf_op jit(solution)/shard_map/vmap(vmap())/gather
  34.5 2.1 %bitcast_dynamic-update-slice_fusion.2 = bf16[32,2,19456]{2,1,0:T(2,128)(2,1)} fusion(bf16[32,2,19456]{2,1,0:T(2,128)(2,1)} %get-tuple-element.97, s32[]{:T(128)} %get-tuple-element.94, bf16[2,32,19584]{2,0,1:T(2,128)(2,1)S(1)} %get-tuple-element.100, s32[]{:T(128)} %bitcast.72, s32[]{:T(128)} %bitcast.73), kind=kLoop, calls=%fused_computation.2.clone.1 | loop fusion | bytes 157184 | tf_op jit(solution)/shard_map/vmap(vmap())/gather
  37.2 2.1 %bitcast_dynamic-update-slice_fusion.2 = bf16[32,2,19456]{2,1,0:T(2,128)(2,1)} fusion(bf16[32,2,19456]{2,1,0:T(2,128)(2,1)} %get-tuple-element.97, s32[]{:T(128)} %get-tuple-element.94, bf16[2,32,19584]{2,0,1:T(2,128)(2,1)S(1)} %get-tuple-element.100, s32[]{:T(128)} %bitcast.72, s32[]{:T(128)} %bitcast.73), kind=kLoop, calls=%fused_computation.2.clone.1 | loop fusion | bytes 157184 | tf_op jit(solution)/shard_map/vmap(vmap())/gather
  39.9 2.1 %bitcast_dynamic-update-slice_fusion.2 = bf16[32,2,19456]{2,1,0:T(2,128)(2,1)} fusion(bf16[32,2,19456]{2,1,0:T(2,128)(2,1)} %get-tuple-element.97, s32[]{:T(128)} %get-tuple-element.94, bf16[2,32,19584]{2,0,1:T(2,128)(2,1)S(1)} %get-tuple-element.100, s32[]{:T(128)} %bitcast.72, s32[]{:T(128)} %bitcast.73), kind=kLoop, calls=%fused_computation.2.clone.1 | loop fusion | bytes 157184 | tf_op jit(solution)/shard_map/vmap(vmap())/gather
  42.6 2.1 %bitcast_dynamic-update-slice_fusion.2 = bf16[32,2,19456]{2,1,0:T(2,128)(2,1)} fusion(bf16[32,2,19456]{2,1,0:T(2,128)(2,1)} %get-tuple-element.97, s32[]{:T(128)} %get-tuple-element.94, bf16[2,32,19584]{2,0,1:T(2,128)(2,1)S(1)} %get-tuple-element.100, s32[]{:T(128)} %bitcast.72, s32[]{:T(128)} %bitcast.73), kind=kLoop, calls=%fused_computation.2.clone.1 | loop fusion | bytes 157184 | tf_op jit(solution)/shard_map/vmap(vmap())/gather
  45.3 2.1 %bitcast_dynamic-update-slice_fusion.2 = bf16[32,2,19456]{2,1,0:T(2,128)(2,1)} fusion(bf16[32,2,19456]{2,1,0:T(2,128)(2,1)} %get-tuple-element.97, s32[]{:T(128)} %get-tuple-element.94, bf16[2,32,19584]{2,0,1:T(2,128)(2,1)S(1)} %get-tuple-element.100, s32[]{:T(128)} %bitcast.72, s32[]{:T(128)} %bitcast.73), kind=kLoop, calls=%fused_computation.2.clone.1 | loop fusion | bytes 157184 | tf_op jit(solution)/shard_map/vmap(vmap())/gather
  48.0 2.1 %bitcast_dynamic-update-slice_fusion.2 = bf16[32,2,19456]{2,1,0:T(2,128)(2,1)} fusion(bf16[32,2,19456]{2,1,0:T(2,128)(2,1)} %get-tuple-element.97, s32[]{:T(128)} %get-tuple-element.94, bf16[2,32,19584]{2,0,1:T(2,128)(2,1)S(1)} %get-tuple-element.100, s32[]{:T(128)} %bitcast.72, s32[]{:T(128)} %bitcast.73), kind=kLoop, calls=%fused_computation.2.clone.1 | loop fusion | bytes 157184 | tf_op jit(solution)/shard_map/vmap(vmap())/gather
  50.6 2.1 %bitcast_dynamic-update-slice_fusion.2 = bf16[32,2,19456]{2,1,0:T(2,128)(2,1)} fusion(bf16[32,2,19456]{2,1,0:T(2,128)(2,1)} %get-tuple-element.97, s32[]{:T(128)} %get-tuple-element.94, bf16[2,32,19584]{2,0,1:T(2,128)(2,1)S(1)} %get-tuple-element.100, s32[]{:T(128)} %bitcast.72, s32[]{:T(128)} %bitcast.73), kind=kLoop, calls=%fused_computation.2.clone.1 | loop fusion | bytes 157184 | tf_op jit(solution)/shard_map/vmap(vmap())/gather
  53.3 2.1 %bitcast_dynamic-update-slice_fusion.2 = bf16[32,2,19456]{2,1,0:T(2,128)(2,1)} fusion(bf16[32,2,19456]{2,1,0:T(2,128)(2,1)} %get-tuple-element.97, s32[]{:T(128)} %get-tuple-element.94, bf16[2,32,19584]{2,0,1:T(2,128)(2,1)S(1)} %get-tuple-element.100, s32[]{:T(128)} %bitcast.72, s32[]{:T(128)} %bitcast.73), kind=kLoop, calls=%fused_computation.2.clone.1 | loop fusion | bytes 157184 | tf_op jit(solution)/shard_map/vmap(vmap())/gather
  56.0 2.1 %bitcast_dynamic-update-slice_fusion.2 = bf16[32,2,19456]{2,1,0:T(2,128)(2,1)} fusion(bf16[32,2,19456]{2,1,0:T(2,128)(2,1)} %get-tuple-element.97, s32[]{:T(128)} %get-tuple-element.94, bf16[2,32,19584]{2,0,1:T(2,128)(2,1)S(1)} %get-tuple-element.100, s32[]{:T(128)} %bitcast.72, s32[]{:T(128)} %bitcast.73), kind=kLoop, calls=%fused_computation.2.clone.1 | loop fusion | bytes 157184 | tf_op jit(solution)/shard_map/vmap(vmap())/gather
  58.7 2.1 %bitcast_dynamic-update-slice_fusion.2 = bf16[32,2,19456]{2,1,0:T(2,128)(2,1)} fusion(bf16[32,2,19456]{2,1,0:T(2,128)(2,1)} %get-tuple-element.97, s32[]{:T(128)} %get-tuple-element.94, bf16[2,32,19584]{2,0,1:T(2,128)(2,1)S(1)} %get-tuple-element.100, s32[]{:T(128)} %bitcast.72, s32[]{:T(128)} %bitcast.73), kind=kLoop, calls=%fused_computation.2.clone.1 | loop fusion | bytes 157184 | tf_op jit(solution)/shard_map/vmap(vmap())/gather
  61.4 2.1 %bitcast_dynamic-update-slice_fusion.2 = bf16[32,2,19456]{2,1,0:T(2,128)(2,1)} fusion(bf16[32,2,19456]{2,1,0:T(2,128)(2,1)} %get-tuple-element.97, s32[]{:T(128)} %get-tuple-element.94, bf16[2,32,19584]{2,0,1:T(2,128)(2,1)S(1)} %get-tuple-element.100, s32[]{:T(128)} %bitcast.72, s32[]{:T(128)} %bitcast.73), kind=kLoop, calls=%fused_computation.2.clone.1 | loop fusion | bytes 157184 | tf_op jit(solution)/shard_map/vmap(vmap())/gather
  64.0 2.1 %bitcast_dynamic-update-slice_fusion.2 = bf16[32,2,19456]{2,1,0:T(2,128)(2,1)} fusion(bf16[32,2,19456]{2,1,0:T(2,128)(2,1)} %get-tuple-element.97, s32[]{:T(128)} %get-tuple-element.94, bf16[2,32,19584]{2,0,1:T(2,128)(2,1)S(1)} %get-tuple-element.100, s32[]{:T(128)} %bitcast.72, s32[]{:T(128)} %bitcast.73), kind=kLoop, calls=%fused_computation.2.clone.1 | loop fusion | bytes 157184 | tf_op jit(solution)/shard_map/vmap(vmap())/gather
  66.7 2.1 %bitcast_dynamic-update-slice_fusion.2 = bf16[32,2,19456]{2,1,0:T(2,128)(2,1)} fusion(bf16[32,2,19456]{2,1,0:T(2,128)(2,1)} %get-tuple-element.97, s32[]{:T(128)} %get-tuple-element.94, bf16[2,32,19584]{2,0,1:T(2,128)(2,1)S(1)} %get-tuple-element.100, s32[]{:T(128)} %bitcast.72, s32[]{:T(128)} %bitcast.73), kind=kLoop, calls=%fused_computation.2.clone.1 | loop fusion | bytes 157184 | tf_op jit(solution)/shard_map/vmap(vmap())/gather
  69.4 2.1 %bitcast_dynamic-update-slice_fusion.2 = bf16[32,2,19456]{2,1,0:T(2,128)(2,1)} fusion(bf16[32,2,19456]{2,1,0:T(2,128)(2,1)} %get-tuple-element.97, s32[]{:T(128)} %get-tuple-element.94, bf16[2,32,19584]{2,0,1:T(2,128)(2,1)S(1)} %get-tuple-element.100, s32[]{:T(128)} %bitcast.72, s32[]{:T(128)} %bitcast.73), kind=kLoop, calls=%fused_computation.2.clone.1 | loop fusion | bytes 157184 | tf_op jit(solution)/shard_map/vmap(vmap())/gather
  72.1 2.1 %bitcast_dynamic-update-slice_fusion.2 = bf16[32,2,19456]{2,1,0:T(2,128)(2,1)} fusion(bf16[32,2,19456]{2,1,0:T(2,128)(2,1)} %get-tuple-element.97, s32[]{:T(128)} %get-tuple-element.94, bf16[2,32,19584]{2,0,1:T(2,128)(2,1)S(1)} %get-tuple-element.100, s32[]{:T(128)} %bitcast.72, s32[]{:T(128)} %bitcast.73), kind=kLoop, calls=%fused_computation.2.clone.1 | loop fusion | bytes 157184 | tf_op jit(solution)/shard_map/vmap(vmap())/gather
  74.7 2.1 %bitcast_dynamic-update-slice_fusion.2 = bf16[32,2,19456]{2,1,0:T(2,128)(2,1)} fusion(bf16[32,2,19456]{2,1,0:T(2,128)(2,1)} %get-tuple-element.97, s32[]{:T(128)} %get-tuple-element.94, bf16[2,32,19584]{2,0,1:T(2,128)(2,1)S(1)} %get-tuple-element.100, s32[]{:T(128)} %bitcast.72, s32[]{:T(128)} %bitcast.73), kind=kLoop, calls=%fused_computation.2.clone.1 | loop fusion | bytes 157184 | tf_op jit(solution)/shard_map/vmap(vmap())/gather
  77.4 2.1 %bitcast_dynamic-update-slice_fusion.2 = bf16[32,2,19456]{2,1,0:T(2,128)(2,1)} fusion(bf16[32,2,19456]{2,1,0:T(2,128)(2,1)} %get-tuple-element.97, s32[]{:T(128)} %get-tuple-element.94, bf16[2,32,19584]{2,0,1:T(2,128)(2,1)S(1)} %get-tuple-element.100, s32[]{:T(128)} %bitcast.72, s32[]{:T(128)} %bitcast.73), kind=kLoop, calls=%fused_computation.2.clone.1 | loop fusion | bytes 157184 | tf_op jit(solution)/shard_map/vmap(vmap())/gather
  80.1 2.1 %bitcast_dynamic-update-slice_fusion.2 = bf16[32,2,19456]{2,1,0:T(2,128)(2,1)} fusion(bf16[32,2,19456]{2,1,0:T(2,128)(2,1)} %get-tuple-element.97, s32[]{:T(128)} %get-tuple-element.94, bf16[2,32,19584]{2,0,1:T(2,128)(2,1)S(1)} %get-tuple-element.100, s32[]{:T(128)} %bitcast.72, s32[]{:T(128)} %bitcast.73), kind=kLoop, calls=%fused_computation.2.clone.1 | loop fusion | bytes 157184 | tf_op jit(solution)/shard_map/vmap(vmap())/gather
  82.8 2.1 %bitcast_dynamic-update-slice_fusion.2 = bf16[32,2,19456]{2,1,0:T(2,128)(2,1)} fusion(bf16[32,2,19456]{2,1,0:T(2,128)(2,1)} %get-tuple-element.97, s32[]{:T(128)} %get-tuple-element.94, bf16[2,32,19584]{2,0,1:T(2,128)(2,1)S(1)} %get-tuple-element.100, s32[]{:T(128)} %bitcast.72, s32[]{:T(128)} %bitcast.73), kind=kLoop, calls=%fused_computation.2.clone.1 | loop fusion | bytes 157184 | tf_op jit(solution)/shard_map/vmap(vmap())/gather
  85.4 2.1 %bitcast_dynamic-update-slice_fusion.2 = bf16[32,2,19456]{2,1,0:T(2,128)(2,1)} fusion(bf16[32,2,19456]{2,1,0:T(2,128)(2,1)} %get-tuple-element.97, s32[]{:T(128)} %get-tuple-element.94, bf16[2,32,19584]{2,0,1:T(2,128)(2,1)S(1)} %get-tuple-element.100, s32[]{:T(128)} %bitcast.72, s32[]{:T(128)} %bitcast.73), kind=kLoop, calls=%fused_computation.2.clone.1 | loop fusion | bytes 157184 | tf_op jit(solution)/shard_map/vmap(vmap())/gather
  88.1 2.1 %bitcast_dynamic-update-slice_fusion.2 = bf16[32,2,19456]{2,1,0:T(2,128)(2,1)} fusion(bf16[32,2,19456]{2,1,0:T(2,128)(2,1)} %get-tuple-element.97, s32[]{:T(128)} %get-tuple-element.94, bf16[2,32,19584]{2,0,1:T(2,128)(2,1)S(1)} %get-tuple-element.100, s32[]{:T(128)} %bitcast.72, s32[]{:T(128)} %bitcast.73), kind=kLoop, calls=%fused_computation.2.clone.1 | loop fusion | bytes 157184 | tf_op jit(solution)/shard_map/vmap(vmap())/gather
  90.8 2.1 %bitcast_dynamic-update-slice_fusion.2 = bf16[32,2,19456]{2,1,0:T(2,128)(2,1)} fusion(bf16[32,2,19456]{2,1,0:T(2,128)(2,1)} %get-tuple-element.97, s32[]{:T(128)} %get-tuple-element.94, bf16[2,32,19584]{2,0,1:T(2,128)(2,1)S(1)} %get-tuple-element.100, s32[]{:T(128)} %bitcast.72, s32[]{:T(128)} %bitcast.73), kind=kLoop, calls=%fused_computation.2.clone.1 | loop fusion | bytes 157184 | tf_op jit(solution)/shard_map/vmap(vmap())/gather
  93.5 2.1 %bitcast_dynamic-update-slice_fusion.2 = bf16[32,2,19456]{2,1,0:T(2,128)(2,1)} fusion(bf16[32,2,19456]{2,1,0:T(2,128)(2,1)} %get-tuple-element.97, s32[]{:T(128)} %get-tuple-element.94, bf16[2,32,19584]{2,0,1:T(2,128)(2,1)S(1)} %get-tuple-element.100, s32[]{:T(128)} %bitcast.72, s32[]{:T(128)} %bitcast.73), kind=kLoop, calls=%fused_computation.2.clone.1 | loop fusion | bytes 157184 | tf_op jit(solution)/shard_map/vmap(vmap())/gather
  96.1 2.1 %bitcast_dynamic-update-slice_fusion.2 = bf16[32,2,19456]{2,1,0:T(2,128)(2,1)} fusion(bf16[32,2,19456]{2,1,0:T(2,128)(2,1)} %get-tuple-element.97, s32[]{:T(128)} %get-tuple-element.94, bf16[2,32,19584]{2,0,1:T(2,128)(2,1)S(1)} %get-tuple-element.100, s32[]{:T(128)} %bitcast.72, s32[]{:T(128)} %bitcast.73), kind=kLoop, calls=%fused_computation.2.clone.1 | loop fusion | bytes 157184 | tf_op jit(solution)/shard_map/vmap(vmap())/gather
  98.8 2.1 %bitcast_dynamic-update-slice_fusion.2 = bf16[32,2,19456]{2,1,0:T(2,128)(2,1)} fusion(bf16[32,2,19456]{2,1,0:T(2,128)(2,1)} %get-tuple-element.97, s32[]{:T(128)} %get-tuple-element.94, bf16[2,32,19584]{2,0,1:T(2,128)(2,1)S(1)} %get-tuple-element.100, s32[]{:T(128)} %bitcast.72, s32[]{:T(128)} %bitcast.73), kind=kLoop, calls=%fused_computation.2.clone.1 | loop fusion | bytes 157184 | tf_op jit(solution)/shard_map/vmap(vmap())/gather
  101.5 2.1 %bitcast_dynamic-update-slice_fusion.2 = bf16[32,2,19456]{2,1,0:T(2,128)(2,1)} fusion(bf16[32,2,19456]{2,1,0:T(2,128)(2,1)} %get-tuple-element.97, s32[]{:T(128)} %get-tuple-element.94, bf16[2,32,19584]{2,0,1:T(2,128)(2,1)S(1)} %get-tuple-element.100, s32[]{:T(128)} %bitcast.72, s32[]{:T(128)} %bitcast.73), kind=kLoop, calls=%fused_computation.2.clone.1 | loop fusion | bytes 157184 | tf_op jit(solution)/shard_map/vmap(vmap())/gather
  104.2 2.1 %bitcast_dynamic-update-slice_fusion.2 = bf16[32,2,19456]{2,1,0:T(2,128)(2,1)} fusion(bf16[32,2,19456]{2,1,0:T(2,128)(2,1)} %get-tuple-element.97, s32[]{:T(128)} %get-tuple-element.94, bf16[2,32,19584]{2,0,1:T(2,128)(2,1)S(1)} %get-tuple-element.100, s32[]{:T(128)} %bitcast.72, s32[]{:T(128)} %bitcast.73), kind=kLoop, calls=%fused_computation.2.clone.1 | loop fusion | bytes 157184 | tf_op jit(solution)/shard_map/vmap(vmap())/gather
  106.2 3.6 %copy.23 = bf16[2,32,19456]{2,1,0:T(8,128)(2,1)} copy(bf16[2,32,19456]{2,0,1:T(2,128)(2,1)} %bitcast.74) | data formatting | bytes 4980736 | tf_op jit(solution)/shard_map/vmap(vmap())/gather | solution.py:17
  109.9 3.3 %reshape.36 = bf16[2,32,19,1024]{3,2,1,0:T(8,128)(2,1)S(1)} reshape(bf16[2,32,19456]{2,1,0:T(8,128)(2,1)} %copy.23) | data formatting | bytes 4980736 | tf_op jit(solution)/shard_map/reshape | solution.py:20
  113.2 5.1 %add_convert_fusion = bf16[2,32,4,1024]{3,2,1,0:T(4,128)(2,1)} fusion(bf16[2,32,19,1024]{3,2,1,0:T(8,128)(2,1)S(1)} %reshape.36, f32[1024]{0:T(1024)S(1)} %bitcast.94, f32[1024]{0:T(1024)S(1)} %bitcast.93, f32[1024]{0:T(1024)S(1)} %bitcast.92, f32[1024]{0:T(1024)S(1)} %bitcast.91, f32[1024]{0:T(1024)S(1)} %bitcast.90, f32[1024]{0:T(1024)S(1)} %bitcast.89, ...), kind=kLoop, calls=%fused_computation.26 | loop fusion | flops 12582912 | bytes 8978432 | tf_op jit(solution)/shard_map/convert_element_type | solution.py:27
  119.5 4.8 %fusion.1 = f32[256,2048]{1,0:T(8,128)S(1)} fusion(bf16[256,1024]{1,0:T(8,128)(2,1)S(1)} %reshape.37, f32[1024,1024]{1,0:T(8,128)} %get-tuple-element.55, f32[1024,1024]{1,0:T(8,128)} %get-tuple-element.56), kind=kOutput, calls=%fused_computation.10 | convolution fusion | flops 1082130432 | bytes 11010048 | tf_op jit(solution)/shard_map/dot_general | solution.py:40
  126.7 2.8 %reshape.38 = f32[2,32,4,2,1024]{4,3,2,1,0:T(2,128)} reshape(f32[256,2048]{1,0:T(8,128)S(1)} %fusion.10) | data formatting | bytes 4194304 | tf_op jit(solution)/shard_map/reshape | solution.py:42
  129.5 5.4 %fusion.17 = (f32[1,32,4,1,1024]{4,3,2,1,0:T(1,128)S(1)}, f32[1,32,4,1,1024]{4,3,2,1,0:T(1,128)S(1)}, f32[1,32,4,1,1024]{4,3,2,1,0:T(1,128)}, f32[1,32,4,1,1024]{4,3,2,1,0:T(1,128)}) fusion(f32[2,32,4,2,1024]{4,3,2,1,0:T(2,128)} %reshape.38), kind=kLoop, calls=%fused_computation.46 | loop fusion | bytes 4194304 | tf_op jit(solution)/shard_map/slice | solution.py:44
  134.9 2.7 %copy.34 = f32[1,32,4,1,1024]{1,2,4,3,0:T(4,128)S(1)} copy(f32[1,32,4,1,1024]{4,3,2,1,0:T(1,128)} %get-tuple-element.36) | data formatting | bytes 1048576
  137.6 3.3 %copy.35 = f32[1,32,4,1,1024]{1,2,4,3,0:T(4,128)} copy(f32[1,32,4,1,1024]{4,3,2,1,0:T(1,128)} %get-tuple-element.35) | data formatting | bytes 1048576
  141.0 2.4 %copy.36 = f32[1,32,4,1,1024]{1,2,4,3,0:T(4,128)} copy(f32[1,32,4,1,1024]{4,3,2,1,0:T(1,128)S(1)} %get-tuple-element.34) | data formatting | bytes 1048576
  143.3 2.4 %copy.37 = f32[1,32,4,1,1024]{1,2,4,3,0:T(4,128)} copy(f32[1,32,4,1,1024]{4,3,2,1,0:T(1,128)S(1)} %get-tuple-element.33) | data formatting | bytes 1048576
  145.8 5.7 %add_reduce_fusion = (f32[32,1024]{0,1:T(8,128)S(1)}, bf16[32,4,1024]{0,1,2:T(4,128)(2,1)}, bf16[32,4,1024]{0,1,2:T(4,128)(2,1)}) fusion(f32[1,32,4,1,1024]{1,2,4,3,0:T(4,128)S(1)} %copy.34, f32[1,32,4,1,1024]{1,2,4,3,0:T(4,128)} %copy.35, f32[1,32,4,1,1024]{1,2,4,3,0:T(4,128)} %copy.36, f32[1,32,4,1,1024]{1,2,4,3,0:T(4,128)} %copy.37), kind=kLoop, calls=%fused_computation.21 | loop fusion | flops 1015808 | bytes 2752512 | tf_op jit(solution)/shard_map/reduce_sum | solution.py:63
  155.8 4.2 %all-to-all-start = ((bf16[4,2,512]{2,1,0:T(2,128)(2,1)}), bf16[4,2,512]{2,1,0:T(2,128)(2,1)S(1)}, u32[]{:S(2)}, u32[]{:S(2)}) async-start(bf16[4,2,512]{2,1,0:T(2,128)(2,1)} %reshape.78), calls=%async_computation | async-start | bytes 16384 | tf_op jit(solution)/shard_map/all_to_all | solution.py:70
  164.0 21.6 %all_gather.3 = bf16[2,4,4,1024]{3,2,1,0:T(4,128)(2,1)S(1)} all-gather(bf16[2,4,4,128]{3,2,1,0:T(4,128)(2,1)S(1)} %all_to_all.16), channel_id=1, replica_groups=mesh['elem'=8,'chan'=4] {'elem'}, dimensions={3}, use_global_device_ids=true | all-gather | bytes 73728 | tf_op jit(solution)/shard_map/all_gather | solution.py:72
  (102 shorter events, 33.3 us)
Async XLA Ops:
  0.6 17.8 %copy-start.3 = (bf16[16,1024]{1,0:T(8,128)(2,1)S(1)}, bf16[16,1024]{1,0:T(8,128)(2,1)}, u32[]{:S(2)}) copy-start(bf16[16,1024]{1,0:T(8,128)(2,1)} %param.7) | copy-start | bytes 98308
  0.7 17.9 %copy-start.2 = (bf16[2,32,19584]{2,1,0:T(8,128)(2,1)S(1)}, bf16[2,32,19584]{2,1,0:T(8,128)(2,1)}, u32[]{:S(2)}) copy-start(bf16[2,32,19584]{2,1,0:T(8,128)(2,1)} %param.5) | copy-start | bytes 7520260
  18.5 2.0 %copy-start.4 = (s32[32]{0:T(128)S(1)}, s32[32]{0:T(128)}, u32[]{:S(2)}) copy-start(s32[32]{0:T(128)} %param.6) | copy-start | bytes 388
  119.5 4.9 %copy-start = (f32[1024,1024]{1,0:T(8,128)S(1)}, f32[1024,1024]{1,0:T(8,128)}, u32[]{:S(2)}) copy-start(f32[1024,1024]{1,0:T(8,128)} %get-tuple-element.55) | copy-start | bytes 12582916
  119.5 5.9 %copy-start.1 = (f32[1024,1024]{1,0:T(8,128)S(1)}, f32[1024,1024]{1,0:T(8,128)}, u32[]{:S(2)}) copy-start(f32[1024,1024]{1,0:T(8,128)} %get-tuple-element.56) | copy-start | bytes 12582916
  137.6 8.1 %copy-start.5 = (s32[16]{0:T(128)S(1)}, s32[16]{0:T(128)}, u32[]{:S(2)}) copy-start(s32[16]{0:T(128)} %param.8) | copy-start | bytes 196
  155.8 8.1 %all-to-all-start = ((bf16[4,2,512]{2,1,0:T(2,128)(2,1)}), bf16[4,2,512]{2,1,0:T(2,128)(2,1)S(1)}, u32[]{:S(2)}, u32[]{:S(2)}) async-start(bf16[4,2,512]{2,1,0:T(2,128)(2,1)} %reshape.78), calls=%async_computation | async-start | bytes 16384 | tf_op jit(solution)/shard_map/all_to_all | solution.py:70
where the time goes:
time: 189 us; the launch traced here: 187 us
  local copies, waits for them, and re-layouts  123 us (65%)
  other arithmetic  29.3 us (16%)
  blocking collectives  21.6 us (11%)
  matrix products  7.36 us (4%)
  starting transfers between devices  4.24 us (2%)
    gather x96, local copies, waits for them, and re-layouts  85.6 us
    all_gather x1, blocking collectives, on_device(): lax.all_gather(turned, 'elem', axis=3, tiled=True)  21.6 us
    mul x1, other arithmetic, spectra(): jnp.sin(radians) * factor  17.8 us
    unnamed x21, local copies, waits for them, and re-layouts  15.3 us
    reduce_sum x1, other arithmetic, on_device(): jnp.mean(spec_real * spec_real + spec_imag * spec_imag, axis=1)  5.67 us
    slice x1, local copies, waits for them, and re-layouts, spectra(): spec_imag = product[1, :, :, 0] - product[0, :, :, 1]  5.38 us
    convert_element_type x1, other arithmetic, filtered(): return running.astype(jnp.bfloat16)  5.1 us
    dot_general x1, matrix products, spectra(): product = jnp.dot(flattened, basis_high, preferred_element_type=jnp.float32)  4.85 us
  transfers between devices with their start and end apart: 1, of which 1 were waited for; matrix products, arithmetic and copies ran while one was open for 1% of the time, Pallas kernels for 0%

commit v1 on v0

--- a/solution.py
+++ b/solution.py
@@ -69,7 +69,11 @@
     picked = jnp.transpose(picked, (0, 3, 2, 1))
     turned = lax.all_to_all(picked, "chan", split_axis=1, concat_axis=3, tiled=True)
     local_beams = beam_weights.shape[0]
-    summed = beam_terms(lax.all_gather(turned, "elem", axis=3, tiled=True), beam_weights)
+
+    def switch_members_all_in(z):
+        return jnp.concatenate(lax.all_gather(z, "elem"), axis=3)
+
+    summed = beam_terms(switch_members_all_in(turned), beam_weights)
     beam_voltages = summed.reshape(2, SUB_C * FRAMES, local_beams)
     return (element_power, beam_voltages)
 

time: 189 us -> 195 us (1.032)
  blocking collectives: 21.6 us -> 31.3 us
  local copies, waits for them, and re-layouts: 123 us -> 120 us
    all_gather x1, blocking collectives: 21.6 us -> 31.3 us  [switch_members_all_in(): return jnp.concatenate(lax.all_gather(z, 'elem'), axis=3)]
    gather x96, local copies, waits for them, and re-layouts: 85.6 us -> 82.8 us
where the time goes in v1:
time: 195 us; the launch traced here: 194 us
  local copies, waits for them, and re-layouts  120 us (62%)
  blocking collectives  31.3 us (16%)
  other arithmetic  29.3 us (15%)
  matrix products  7.36 us (4%)
  starting transfers between devices  4.24 us (2%)
    gather x96, local copies, waits for them, and re-layouts  82.8 us
    all_gather x1, blocking collectives, switch_members_all_in(): return jnp.concatenate(lax.all_gather(z, 'elem'), axis=3)  31.3 us
    mul x1, other arithmetic, spectra(): jnp.sin(radians) * factor  17.8 us
    unnamed x21, local copies, waits for them, and re-layouts  15.3 us
    reduce_sum x1, other arithmetic, on_device(): jnp.mean(spec_real * spec_real + spec_imag * spec_imag, axis=1)  5.68 us
    slice x1, local copies, waits for them, and re-layouts, spectra(): spec_imag = product[1, :, :, 0] - product[0, :, :, 1]  5.37 us
    convert_element_type x1, other arithmetic, filtered(): return running.astype(jnp.bfloat16)  5.1 us
    dot_general x1, matrix products, spectra(): product = jnp.dot(flattened, basis_high, preferred_element_type=jnp.float32)  4.85 us
  transfers between devices with their start and end apart: 1, of which 1 were waited for; matrix products, arithmetic and copies ran while one was open for 1% of the time, Pallas kernels for 0%

profile of v1, /device:TPU:0, one launch (start us, length us, event | category | flops | bytes accessed | tf_op | source)
XLA Modules:
  0.0 194.4 jit_solution(5556805223871747941)
XLA Ops:
  0.7 17.8 %sine_multiply_fusion = (f32[1024,1024]{1,0:T(8,128)}, f32[1024,1024]{1,0:T(8,128)}) fusion(), kind=kLoop, calls=%fused_computation.14 | loop fusion | flops 16777216 | bytes 8388608 | tf_op jit(solution)/shard_map/mul | solution.py:36
  18.5 1.9 copy.24
  20.5 82.9 %while.1 = (s32[]{:T(128)}, bf16[2,32,19584]{2,0,1:T(2,128)(2,1)S(1)}, s32[32,2]{0,1:T(2,128)S(1)}, bf16[32,2,19456]{2,1,0:T(2,128)(2,1)}, s32[]{:T(128)}) while((s32[]{:T(128)}, bf16[2,32,19584]{2,0,1:T(2,128)(2,1)S(1)}, s32[32,2]{0,1:T(2,128)S(1)}, bf16[32,2,19456]{2,1,0:T(2,128)(2,1)}, s32[]{:T(128)}) %tuple.50), condition=%wide.while_cond, body=%wide.while_body.sunk | while | flops 2 | bytes 157281 | solution.py:17
  21.1 2.0 %bitcast_dynamic-update-slice_fusion.2 = bf16[32,2,19456]{2,1,0:T(2,128)(2,1)} fusion(bf16[32,2,19456]{2,1,0:T(2,128)(2,1)} %get-tuple-element.99, s32[]{:T(128)} %get-tuple-element.96, bf16[2,32,19584]{2,0,1:T(2,128)(2,1)S(1)} %get-tuple-element.102, s32[]{:T(128)} %bitcast.73, s32[]{:T(128)} %bitcast.74), kind=kLoop, calls=%fused_computation.2.clone.1 | loop fusion | bytes 157184 | tf_op jit(solution)/shard_map/vmap(vmap())/gather
  23.7 2.0 %bitcast_dynamic-update-slice_fusion.2 = bf16[32,2,19456]{2,1,0:T(2,128)(2,1)} fusion(bf16[32,2,19456]{2,1,0:T(2,128)(2,1)} %get-tuple-element.99, s32[]{:T(128)} %get-tuple-element.96, bf16[2,32,19584]{2,0,1:T(2,128)(2,1)S(1)} %get-tuple-element.102, s32[]{:T(128)} %bitcast.73, s32[]{:T(128)} %bitcast.74), kind=kLoop, calls=%fused_computation.2.clone.1 | loop fusion | bytes 157184 | tf_op jit(solution)/shard_map/vmap(vmap())/gather
  26.3 2.0 %bitcast_dynamic-update-slice_fusion.2 = bf16[32,2,19456]{2,1,0:T(2,128)(2,1)} fusion(bf16[32,2,19456]{2,1,0:T(2,128)(2,1)} %get-tuple-element.99, s32[]{:T(128)} %get-tuple-element.96, bf16[2,32,19584]{2,0,1:T(2,128)(2,1)S(1)} %get-tuple-element.102, s32[]{:T(128)} %bitcast.73, s32[]{:T(128)} %bitcast.74), kind=kLoop, calls=%fused_computation.2.clone.1 | loop fusion | bytes 157184 | tf_op jit(solution)/shard_map/vmap(vmap())/gather
  28.9 2.0 %bitcast_dynamic-update-slice_fusion.2 = bf16[32,2,19456]{2,1,0:T(2,128)(2,1)} fusion(bf16[32,2,19456]{2,1,0:T(2,128)(2,1)} %get-tuple-element.99, s32[]{:T(128)} %get-tuple-element.96, bf16[2,32,19584]{2,0,1:T(2,128)(2,1)S(1)} %get-tuple-element.102, s32[]{:T(128)} %bitcast.73, s32[]{:T(128)} %bitcast.74), kind=kLoop, calls=%fused_computation.2.clone.1 | loop fusion | bytes 157184 | tf_op jit(solution)/shard_map/vmap(vmap())/gather
  31.5 2.0 %bitcast_dynamic-update-slice_fusion.2 = bf16[32,2,19456]{2,1,0:T(2,128)(2,1)} fusion(bf16[32,2,19456]{2,1,0:T(2,128)(2,1)} %get-tuple-element.99, s32[]{:T(128)} %get-tuple-element.96, bf16[2,32,19584]{2,0,1:T(2,128)(2,1)S(1)} %get-tuple-element.102, s32[]{:T(128)} %bitcast.73, s32[]{:T(128)} %bitcast.74), kind=kLoop, calls=%fused_computation.2.clone.1 | loop fusion | bytes 157184 | tf_op jit(solution)/shard_map/vmap(vmap())/gather
  34.1 2.0 %bitcast_dynamic-update-slice_fusion.2 = bf16[32,2,19456]{2,1,0:T(2,128)(2,1)} fusion(bf16[32,2,19456]{2,1,0:T(2,128)(2,1)} %get-tuple-element.99, s32[]{:T(128)} %get-tuple-element.96, bf16[2,32,19584]{2,0,1:T(2,128)(2,1)S(1)} %get-tuple-element.102, s32[]{:T(128)} %bitcast.73, s32[]{:T(128)} %bitcast.74), kind=kLoop, calls=%fused_computation.2.clone.1 | loop fusion | bytes 157184 | tf_op jit(solution)/shard_map/vmap(vmap())/gather
  36.7 2.0 %bitcast_dynamic-update-slice_fusion.2 = bf16[32,2,19456]{2,1,0:T(2,128)(2,1)} fusion(bf16[32,2,19456]{2,1,0:T(2,128)(2,1)} %get-tuple-element.99, s32[]{:T(128)} %get-tuple-element.96, bf16[2,32,19584]{2,0,1:T(2,128)(2,1)S(1)} %get-tuple-element.102, s32[]{:T(128)} %bitcast.73, s32[]{:T(128)} %bitcast.74), kind=kLoop, calls=%fused_computation.2.clone.1 | loop fusion | bytes 157184 | tf_op jit(solution)/shard_map/vmap(vmap())/gather
  39.3 2.0 %bitcast_dynamic-update-slice_fusion.2 = bf16[32,2,19456]{2,1,0:T(2,128)(2,1)} fusion(bf16[32,2,19456]{2,1,0:T(2,128)(2,1)} %get-tuple-element.99, s32[]{:T(128)} %get-tuple-element.96, bf16[2,32,19584]{2,0,1:T(2,128)(2,1)S(1)} %get-tuple-element.102, s32[]{:T(128)} %bitcast.73, s32[]{:T(128)} %bitcast.74), kind=kLoop, calls=%fused_computation.2.clone.1 | loop fusion | bytes 157184 | tf_op jit(solution)/shard_map/vmap(vmap())/gather
  41.9 2.0 %bitcast_dynamic-update-slice_fusion.2 = bf16[32,2,19456]{2,1,0:T(2,128)(2,1)} fusion(bf16[32,2,19456]{2,1,0:T(2,128)(2,1)} %get-tuple-element.99, s32[]{:T(128)} %get-tuple-element.96, bf16[2,32,19584]{2,0,1:T(2,128)(2,1)S(1)} %get-tuple-element.102, s32[]{:T(128)} %bitcast.73, s32[]{:T(128)} %bitcast.74), kind=kLoop, calls=%fused_computation.2.clone.1 | loop fusion | bytes 157184 | tf_op jit(solution)/shard_map/vmap(vmap())/gather
  44.5 2.0 %bitcast_dynamic-update-slice_fusion.2 = bf16[32,2,19456]{2,1,0:T(2,128)(2,1)} fusion(bf16[32,2,19456]{2,1,0:T(2,128)(2,1)} %get-tuple-element.99, s32[]{:T(128)} %get-tuple-element.96, bf16[2,32,19584]{2,0,1:T(2,128)(2,1)S(1)} %get-tuple-element.102, s32[]{:T(128)} %bitcast.73, s32[]{:T(128)} %bitcast.74), kind=kLoop, calls=%fused_computation.2.clone.1 | loop fusion | bytes 157184 | tf_op jit(solution)/shard_map/vmap(vmap())/gather
  47.1 2.0 %bitcast_dynamic-update-slice_fusion.2 = bf16[32,2,19456]{2,1,0:T(2,128)(2,1)} fusion(bf16[32,2,19456]{2,1,0:T(2,128)(2,1)} %get-tuple-element.99, s32[]{:T(128)} %get-tuple-element.96, bf16[2,32,19584]{2,0,1:T(2,128)(2,1)S(1)} %get-tuple-element.102, s32[]{:T(128)} %bitcast.73, s32[]{:T(128)} %bitcast.74), kind=kLoop, calls=%fused_computation.2.clone.1 | loop fusion | bytes 157184 | tf_op jit(solution)/shard_map/vmap(vmap())/gather
  49.6 2.0 %bitcast_dynamic-update-slice_fusion.2 = bf16[32,2,19456]{2,1,0:T(2,128)(2,1)} fusion(bf16[32,2,19456]{2,1,0:T(2,128)(2,1)} %get-tuple-element.99, s32[]{:T(128)} %get-tuple-element.96, bf16[2,32,19584]{2,0,1:T(2,128)(2,1)S(1)} %get-tuple-element.102, s32[]{:T(128)} %bitcast.73, s32[]{:T(128)} %bitcast.74), kind=kLoop, calls=%fused_computation.2.clone.1 | loop fusion | bytes 157184 | tf_op jit(solution)/shard_map/vmap(vmap())/gather
  52.2 2.0 %bitcast_dynamic-update-slice_fusion.2 = bf16[32,2,19456]{2,1,0:T(2,128)(2,1)} fusion(bf16[32,2,19456]{2,1,0:T(2,128)(2,1)} %get-tuple-element.99, s32[]{:T(128)} %get-tuple-element.96, bf16[2,32,19584]{2,0,1:T(2,128)(2,1)S(1)} %get-tuple-element.102, s32[]{:T(128)} %bitcast.73, s32[]{:T(128)} %bitcast.74), kind=kLoop, calls=%fused_computation.2.clone.1 | loop fusion | bytes 157184 | tf_op jit(solution)/shard_map/vmap(vmap())/gather
  54.8 2.0 %bitcast_dynamic-update-slice_fusion.2 = bf16[32,2,19456]{2,1,0:T(2,128)(2,1)} fusion(bf16[32,2,19456]{2,1,0:T(2,128)(2,1)} %get-tuple-element.99, s32[]{:T(128)} %get-tuple-element.96, bf16[2,32,19584]{2,0,1:T(2,128)(2,1)S(1)} %get-tuple-element.102, s32[]{:T(128)} %bitcast.73, s32[]{:T(128)} %bitcast.74), kind=kLoop, calls=%fused_computation.2.clone.1 | loop fusion | bytes 157184 | tf_op jit(solution)/shard_map/vmap(vmap())/gather
  57.4 2.0 %bitcast_dynamic-update-slice_fusion.2 = bf16[32,2,19456]{2,1,0:T(2,128)(2,1)} fusion(bf16[32,2,19456]{2,1,0:T(2,128)(2,1)} %get-tuple-element.99, s32[]{:T(128)} %get-tuple-element.96, bf16[2,32,19584]{2,0,1:T(2,128)(2,1)S(1)} %get-tuple-element.102, s32[]{:T(128)} %bitcast.73, s32[]{:T(128)} %bitcast.74), kind=kLoop, calls=%fused_computation.2.clone.1 | loop fusion | bytes 157184 | tf_op jit(solution)/shard_map/vmap(vmap())/gather
  60.0 2.0 %bitcast_dynamic-update-slice_fusion.2 = bf16[32,2,19456]{2,1,0:T(2,128)(2,1)} fusion(bf16[32,2,19456]{2,1,0:T(2,128)(2,1)} %get-tuple-element.99, s32[]{:T(128)} %get-tuple-element.96, bf16[2,32,19584]{2,0,1:T(2,128)(2,1)S(1)} %get-tuple-element.102, s32[]{:T(128)} %bitcast.73, s32[]{:T(128)} %bitcast.74), kind=kLoop, calls=%fused_computation.2.clone.1 | loop fusion | bytes 157184 | tf_op jit(solution)/shard_map/vmap(vmap())/gather
  62.6 2.0 %bitcast_dynamic-update-slice_fusion.2 = bf16[32,2,19456]{2,1,0:T(2,128)(2,1)} fusion(bf16[32,2,19456]{2,1,0:T(2,128)(2,1)} %get-tuple-element.99, s32[]{:T(128)} %get-tuple-element.96, bf16[2,32,19584]{2,0,1:T(2,128)(2,1)S(1)} %get-tuple-element.102, s32[]{:T(128)} %bitcast.73, s32[]{:T(128)} %bitcast.74), kind=kLoop, calls=%fused_computation.2.clone.1 | loop fusion | bytes 157184 | tf_op jit(solution)/shard_map/vmap(vmap())/gather
  65.2 2.0 %bitcast_dynamic-update-slice_fusion.2 = bf16[32,2,19456]{2,1,0:T(2,128)(2,1)} fusion(bf16[32,2,19456]{2,1,0:T(2,128)(2,1)} %get-tuple-element.99, s32[]{:T(128)} %get-tuple-element.96, bf16[2,32,19584]{2,0,1:T(2,128)(2,1)S(1)} %get-tuple-element.102, s32[]{:T(128)} %bitcast.73, s32[]{:T(128)} %bitcast.74), kind=kLoop, calls=%fused_computation.2.clone.1 | loop fusion | bytes 157184 | tf_op jit(solution)/shard_map/vmap(vmap())/gather
  67.8 2.0 %bitcast_dynamic-update-slice_fusion.2 = bf16[32,2,19456]{2,1,0:T(2,128)(2,1)} fusion(bf16[32,2,19456]{2,1,0:T(2,128)(2,1)} %get-tuple-element.99, s32[]{:T(128)} %get-tuple-element.96, bf16[2,32,19584]{2,0,1:T(2,128)(2,1)S(1)} %get-tuple-element.102, s32[]{:T(128)} %bitcast.73, s32[]{:T(128)} %bitcast.74), kind=kLoop, calls=%fused_computation.2.clone.1 | loop fusion | bytes 157184 | tf_op jit(solution)/shard_map/vmap(vmap())/gather
  70.3 2.0 %bitcast_dynamic-update-slice_fusion.2 = bf16[32,2,19456]{2,1,0:T(2,128)(2,1)} fusion(bf16[32,2,19456]{2,1,0:T(2,128)(2,1)} %get-tuple-element.99, s32[]{:T(128)} %get-tuple-element.96, bf16[2,32,19584]{2,0,1:T(2,128)(2,1)S(1)} %get-tuple-element.102, s32[]{:T(128)} %bitcast.73, s32[]{:T(128)} %bitcast.74), kind=kLoop, calls=%fused_computation.2.clone.1 | loop fusion | bytes 157184 | tf_op jit(solution)/shard_map/vmap(vmap())/gather
  72.9 2.0 %bitcast_dynamic-update-slice_fusion.2 = bf16[32,2,19456]{2,1,0:T(2,128)(2,1)} fusion(bf16[32,2,19456]{2,1,0:T(2,128)(2,1)} %get-tuple-element.99, s32[]{:T(128)} %get-tuple-element.96, bf16[2,32,19584]{2,0,1:T(2,128)(2,1)S(1)} %get-tuple-element.102, s32[]{:T(128)} %bitcast.73, s32[]{:T(128)} %bitcast.74), kind=kLoop, calls=%fused_computation.2.clone.1 | loop fusion | bytes 157184 | tf_op jit(solution)/shard_map/vmap(vmap())/gather
  75.5 2.0 %bitcast_dynamic-update-slice_fusion.2 = bf16[32,2,19456]{2,1,0:T(2,128)(2,1)} fusion(bf16[32,2,19456]{2,1,0:T(2,128)(2,1)} %get-tuple-element.99, s32[]{:T(128)} %get-tuple-element.96, bf16[2,32,19584]{2,0,1:T(2,128)(2,1)S(1)} %get-tuple-element.102, s32[]{:T(128)} %bitcast.73, s32[]{:T(128)} %bitcast.74), kind=kLoop, calls=%fused_computation.2.clone.1 | loop fusion | bytes 157184 | tf_op jit(solution)/shard_map/vmap(vmap())/gather
  78.1 2.0 %bitcast_dynamic-update-slice_fusion.2 = bf16[32,2,19456]{2,1,0:T(2,128)(2,1)} fusion(bf16[32,2,19456]{2,1,0:T(2,128)(2,1)} %get-tuple-element.99, s32[]{:T(128)} %get-tuple-element.96, bf16[2,32,19584]{2,0,1:T(2,128)(2,1)S(1)} %get-tuple-element.102, s32[]{:T(128)} %bitcast.73, s32[]{:T(128)} %bitcast.74), kind=kLoop, calls=%fused_computation.2.clone.1 | loop fusion | bytes 157184 | tf_op jit(solution)/shard_map/vmap(vmap())/gather
  80.7 2.0 %bitcast_dynamic-update-slice_fusion.2 = bf16[32,2,19456]{2,1,0:T(2,128)(2,1)} fusion(bf16[32,2,19456]{2,1,0:T(2,128)(2,1)} %get-tuple-element.99, s32[]{:T(128)} %get-tuple-element.96, bf16[2,32,19584]{2,0,1:T(2,128)(2,1)S(1)} %get-tuple-element.102, s32[]{:T(128)} %bitcast.73, s32[]{:T(128)} %bitcast.74), kind=kLoop, calls=%fused_computation.2.clone.1 | loop fusion | bytes 157184 | tf_op jit(solution)/shard_map/vmap(vmap())/gather
  83.3 2.0 %bitcast_dynamic-update-slice_fusion.2 = bf16[32,2,19456]{2,1,0:T(2,128)(2,1)} fusion(bf16[32,2,19456]{2,1,0:T(2,128)(2,1)} %get-tuple-element.99, s32[]{:T(128)} %get-tuple-element.96, bf16[2,32,19584]{2,0,1:T(2,128)(2,1)S(1)} %get-tuple-element.102, s32[]{:T(128)} %bitcast.73, s32[]{:T(128)} %bitcast.74), kind=kLoop, calls=%fused_computation.2.clone.1 | loop fusion | bytes 157184 | tf_op jit(solution)/shard_map/vmap(vmap())/gather
  85.9 2.0 %bitcast_dynamic-update-slice_fusion.2 = bf16[32,2,19456]{2,1,0:T(2,128)(2,1)} fusion(bf16[32,2,19456]{2,1,0:T(2,128)(2,1)} %get-tuple-element.99, s32[]{:T(128)} %get-tuple-element.96, bf16[2,32,19584]{2,0,1:T(2,128)(2,1)S(1)} %get-tuple-element.102, s32[]{:T(128)} %bitcast.73, s32[]{:T(128)} %bitcast.74), kind=kLoop, calls=%fused_computation.2.clone.1 | loop fusion | bytes 157184 | tf_op jit(solution)/shard_map/vmap(vmap())/gather
  88.5 2.0 %bitcast_dynamic-update-slice_fusion.2 = bf16[32,2,19456]{2,1,0:T(2,128)(2,1)} fusion(bf16[32,2,19456]{2,1,0:T(2,128)(2,1)} %get-tuple-element.99, s32[]{:T(128)} %get-tuple-element.96, bf16[2,32,19584]{2,0,1:T(2,128)(2,1)S(1)} %get-tuple-element.102, s32[]{:T(128)} %bitcast.73, s32[]{:T(128)} %bitcast.74), kind=kLoop, calls=%fused_computation.2.clone.1 | loop fusion | bytes 157184 | tf_op jit(solution)/shard_map/vmap(vmap())/gather
  91.1 2.0 %bitcast_dynamic-update-slice_fusion.2 = bf16[32,2,19456]{2,1,0:T(2,128)(2,1)} fusion(bf16[32,2,19456]{2,1,0:T(2,128)(2,1)} %get-tuple-element.99, s32[]{:T(128)} %get-tuple-element.96, bf16[2,32,19584]{2,0,1:T(2,128)(2,1)S(1)} %get-tuple-element.102, s32[]{:T(128)} %bitcast.73, s32[]{:T(128)} %bitcast.74), kind=kLoop, calls=%fused_computation.2.clone.1 | loop fusion | bytes 157184 | tf_op jit(solution)/shard_map/vmap(vmap())/gather
  93.6 2.0 %bitcast_dynamic-update-slice_fusion.2 = bf16[32,2,19456]{2,1,0:T(2,128)(2,1)} fusion(bf16[32,2,19456]{2,1,0:T(2,128)(2,1)} %get-tuple-element.99, s32[]{:T(128)} %get-tuple-element.96, bf16[2,32,19584]{2,0,1:T(2,128)(2,1)S(1)} %get-tuple-element.102, s32[]{:T(128)} %bitcast.73, s32[]{:T(128)} %bitcast.74), kind=kLoop, calls=%fused_computation.2.clone.1 | loop fusion | bytes 157184 | tf_op jit(solution)/shard_map/vmap(vmap())/gather
  96.2 2.0 %bitcast_dynamic-update-slice_fusion.2 = bf16[32,2,19456]{2,1,0:T(2,128)(2,1)} fusion(bf16[32,2,19456]{2,1,0:T(2,128)(2,1)} %get-tuple-element.99, s32[]{:T(128)} %get-tuple-element.96, bf16[2,32,19584]{2,0,1:T(2,128)(2,1)S(1)} %get-tuple-element.102, s32[]{:T(128)} %bitcast.73, s32[]{:T(128)} %bitcast.74), kind=kLoop, calls=%fused_computation.2.clone.1 | loop fusion | bytes 157184 | tf_op jit(solution)/shard_map/vmap(vmap())/gather
  98.8 2.0 %bitcast_dynamic-update-slice_fusion.2 = bf16[32,2,19456]{2,1,0:T(2,128)(2,1)} fusion(bf16[32,2,19456]{2,1,0:T(2,128)(2,1)} %get-tuple-element.99, s32[]{:T(128)} %get-tuple-element.96, bf16[2,32,19584]{2,0,1:T(2,128)(2,1)S(1)} %get-tuple-element.102, s32[]{:T(128)} %bitcast.73, s32[]{:T(128)} %bitcast.74), kind=kLoop, calls=%fused_computation.2.clone.1 | loop fusion | bytes 157184 | tf_op jit(solution)/shard_map/vmap(vmap())/gather
  101.4 2.0 %bitcast_dynamic-update-slice_fusion.2 = bf16[32,2,19456]{2,1,0:T(2,128)(2,1)} fusion(bf16[32,2,19456]{2,1,0:T(2,128)(2,1)} %get-tuple-element.99, s32[]{:T(128)} %get-tuple-element.96, bf16[2,32,19584]{2,0,1:T(2,128)(2,1)S(1)} %get-tuple-element.102, s32[]{:T(128)} %bitcast.73, s32[]{:T(128)} %bitcast.74), kind=kLoop, calls=%fused_computation.2.clone.1 | loop fusion | bytes 157184 | tf_op jit(solution)/shard_map/vmap(vmap())/gather
  103.4 3.6 %copy.25 = bf16[2,32,19456]{2,1,0:T(8,128)(2,1)} copy(bf16[2,32,19456]{2,0,1:T(2,128)(2,1)} %bitcast.75) | data formatting | bytes 4980736 | tf_op jit(solution)/shard_map/vmap(vmap())/gather | solution.py:17
  107.0 3.3 %reshape.45 = bf16[2,32,19,1024]{3,2,1,0:T(8,128)(2,1)S(1)} reshape(bf16[2,32,19456]{2,1,0:T(8,128)(2,1)} %copy.25) | data formatting | bytes 4980736 | tf_op jit(solution)/shard_map/reshape | solution.py:20
  110.4 5.1 %add_convert_fusion = bf16[2,32,4,1024]{3,2,1,0:T(4,128)(2,1)} fusion(bf16[2,32,19,1024]{3,2,1,0:T(8,128)(2,1)S(1)} %reshape.45, f32[1024]{0:T(1024)S(1)} %bitcast.96, f32[1024]{0:T(1024)S(1)} %bitcast.95, f32[1024]{0:T(1024)S(1)} %bitcast.94, f32[1024]{0:T(1024)S(1)} %bitcast.93, f32[1024]{0:T(1024)S(1)} %bitcast.92, f32[1024]{0:T(1024)S(1)} %bitcast.91, ...), kind=kLoop, calls=%fused_computation.26 | loop fusion | flops 12582912 | bytes 8978432 | tf_op jit(solution)/shard_map/convert_element_type | solution.py:27
  116.6 4.8 %fusion.1 = f32[256,2048]{1,0:T(8,128)S(1)} fusion(bf16[256,1024]{1,0:T(8,128)(2,1)S(1)} %reshape.46, f32[1024,1024]{1,0:T(8,128)} %get-tuple-element.57, f32[1024,1024]{1,0:T(8,128)} %get-tuple-element.58), kind=kOutput, calls=%fused_computation.10 | convolution fusion | flops 1082130432 | bytes 11010048 | tf_op jit(solution)/shard_map/dot_general | solution.py:40
  123.9 2.8 %reshape.47 = f32[2,32,4,2,1024]{4,3,2,1,0:T(2,128)} reshape(f32[256,2048]{1,0:T(8,128)S(1)} %fusion.10) | data formatting | bytes 4194304 | tf_op jit(solution)/shard_map/reshape | solution.py:42
  126.7 5.4 %fusion.17 = (f32[1,32,4,1,1024]{4,3,2,1,0:T(1,128)S(1)}, f32[1,32,4,1,1024]{4,3,2,1,0:T(1,128)S(1)}, f32[1,32,4,1,1024]{4,3,2,1,0:T(1,128)}, f32[1,32,4,1,1024]{4,3,2,1,0:T(1,128)}) fusion(f32[2,32,4,2,1024]{4,3,2,1,0:T(2,128)} %reshape.47), kind=kLoop, calls=%fused_computation.44 | loop fusion | bytes 4194304 | tf_op jit(solution)/shard_map/slice | solution.py:44
  132.1 2.7 %copy.38 = f32[1,32,4,1,1024]{1,2,4,3,0:T(4,128)S(1)} copy(f32[1,32,4,1,1024]{4,3,2,1,0:T(1,128)} %get-tuple-element.36) | data formatting | bytes 1048576
  134.8 3.3 %copy.39 = f32[1,32,4,1,1024]{1,2,4,3,0:T(4,128)} copy(f32[1,32,4,1,1024]{4,3,2,1,0:T(1,128)} %get-tuple-element.35) | data formatting | bytes 1048576
  138.1 2.4 %copy.40 = f32[1,32,4,1,1024]{1,2,4,3,0:T(4,128)} copy(f32[1,32,4,1,1024]{4,3,2,1,0:T(1,128)S(1)} %get-tuple-element.34) | data formatting | bytes 1048576
  140.5 2.4 %copy.41 = f32[1,32,4,1,1024]{1,2,4,3,0:T(4,128)} copy(f32[1,32,4,1,1024]{4,3,2,1,0:T(1,128)S(1)} %get-tuple-element.33) | data formatting | bytes 1048576
  142.9 5.7 %add_reduce_fusion = (f32[32,1024]{0,1:T(8,128)S(1)}, bf16[32,4,1024]{0,1,2:T(4,128)(2,1)}, bf16[32,4,1024]{0,1,2:T(4,128)(2,1)}) fusion(f32[1,32,4,1,1024]{1,2,4,3,0:T(4,128)S(1)} %copy.38, f32[1,32,4,1,1024]{1,2,4,3,0:T(4,128)} %copy.39, f32[1,32,4,1,1024]{1,2,4,3,0:T(4,128)} %copy.40, f32[1,32,4,1,1024]{1,2,4,3,0:T(4,128)} %copy.41), kind=kLoop, calls=%fused_computation.21 | loop fusion | flops 1015808 | bytes 2752512 | tf_op jit(solution)/shard_map/reduce_sum | solution.py:63
  152.9 4.2 %all-to-all-start = ((bf16[4,2,512]{2,1,0:T(2,128)(2,1)}), bf16[4,2,512]{2,1,0:T(2,128)(2,1)S(1)}, u32[]{:S(2)}, u32[]{:S(2)}) async-start(bf16[4,2,512]{2,1,0:T(2,128)(2,1)} %reshape.88), calls=%async_computation | async-start | bytes 16384 | tf_op jit(solution)/shard_map/all_to_all | solution.py:70
  161.2 31.3 %all_gather.7 = bf16[8,2,4,4,128]{4,3,2,1,0:T(4,128)(2,1)S(1)} all-gather(bf16[1,2,4,4,128]{4,3,2,1,0:T(4,128)(2,1)S(1)} %all_gather.6), channel_id=1, replica_groups=mesh['elem'=8,'chan'=4] {'elem'}, dimensions={0}, use_global_device_ids=true | all-gather | bytes 73728 | tf_op jit(solution)/shard_map/all_gather | solution.py:74
  (107 shorter events, 32.8 us)
Async XLA Ops:
  0.6 17.8 %copy-start.3 = (bf16[16,1024]{1,0:T(8,128)(2,1)S(1)}, bf16[16,1024]{1,0:T(8,128)(2,1)}, u32[]{:S(2)}) copy-start(bf16[16,1024]{1,0:T(8,128)(2,1)} %param.7) | copy-start | bytes 98308
  0.7 17.9 %copy-start.2 = (bf16[2,32,19584]{2,1,0:T(8,128)(2,1)S(1)}, bf16[2,32,19584]{2,1,0:T(8,128)(2,1)}, u32[]{:S(2)}) copy-start(bf16[2,32,19584]{2,1,0:T(8,128)(2,1)} %param.5) | copy-start | bytes 7520260
  18.5 2.0 %copy-start.4 = (s32[32]{0:T(128)S(1)}, s32[32]{0:T(128)}, u32[]{:S(2)}) copy-start(s32[32]{0:T(128)} %param.6) | copy-start | bytes 388
  116.6 4.9 %copy-start = (f32[1024,1024]{1,0:T(8,128)S(1)}, f32[1024,1024]{1,0:T(8,128)}, u32[]{:S(2)}) copy-start(f32[1024,1024]{1,0:T(8,128)} %get-tuple-element.57) | copy-start | bytes 12582916
  116.6 5.9 %copy-start.1 = (f32[1024,1024]{1,0:T(8,128)S(1)}, f32[1024,1024]{1,0:T(8,128)}, u32[]{:S(2)}) copy-start(f32[1024,1024]{1,0:T(8,128)} %get-tuple-element.58) | copy-start | bytes 12582916
  134.8 8.1 %copy-start.5 = (s32[16]{0:T(128)S(1)}, s32[16]{0:T(128)}, u32[]{:S(2)}) copy-start(s32[16]{0:T(128)} %param.8) | copy-start | bytes 196
  152.9 8.1 %all-to-all-start = ((bf16[4,2,512]{2,1,0:T(2,128)(2,1)}), bf16[4,2,512]{2,1,0:T(2,128)(2,1)S(1)}, u32[]{:S(2)}, u32[]{:S(2)}) async-start(bf16[4,2,512]{2,1,0:T(2,128)(2,1)} %reshape.88), calls=%async_computation | async-start | bytes 16384 | tf_op jit(solution)/shard_map/all_to_all | solution.py:70
